TPU v7x, 32 devices: a whole 2x2x4 slice. The times are simulated.
32 devices in a mesh: blk: 8 (over z, y), grp: 4 (over x, core).
Axes of the slice: x: 2, y: 2, z: 4, core: 2. Of those that a mesh axis runs over, the one named last changes fastest.
Arguments:
- image_emb: bfloat16 [12288, 1152], P(('blk', 'grp')), may hold values from -0.1875 to 0.1875
- text_emb: bfloat16 [12288, 1152], P(('blk', 'grp')), may hold values from -0.1875 to 0.1875
- positives: int32 [32, 384], P(('blk', 'grp')), may hold values from 0 to 383, each once within a row
- pair_mask: int32 [8, 7], replicated, may hold values from 0 to 1, as said below
- log_scale: float32 [1], replicated, may hold values from 1.5 to 2.5
- bias: float32 [1], replicated, may hold values from -3 to -1
Outputs:
- image_grad: bfloat16 [12288, 1152], P(('blk', 'grp'))
- text_grad: bfloat16 [12288, 1152], P(('blk', 'grp'))
- loss: float32 [1], replicated
Inputs may be any that keep to these rules, and one draw needn't show every extreme that they name: `positives`: every row is a permutation of the rows of a block. `pair_mask`: column 3 is 1 in every row (each image block is scored against its own text block); at least one row is all ones.
All inputs are finite; a program needn't handle non-finite values.
Results may differ from a plain program's by a relative error of at most 0.0063.
Values may be sent and summed in bfloat16 or wider, within the bound.
A program may use at most 64 MiB of HBM per device.

v0:
```python
import jax
import jax.numpy as jnp
from jax import lax
from jax.sharding import PartitionSpec as P

epsilon = 1e-06


def passed_along(value, axis, steps):
    count = lax.axis_size(axis)
    pairs = [(source, (source + steps) % count) for source in range(count)]
    return lax.ppermute(value, axis, pairs)


def unit_rows(embedded):
    values = embedded.astype(jnp.float32)
    length = jnp.sqrt(jnp.sum(values * values, axis=1, keepdims=True) + epsilon)
    return (values / length, length)


def back_rows(normed, length, upstream):
    inward = jnp.sum(normed * upstream, axis=1, keepdims=True)
    return (upstream - normed * inward) / length


def score_tile(image_side, text_side, labels, logit_scale, offset):
    similar = jnp.einsum("rd,cd->rc", image_side, text_side, preferred_element_type=jnp.float32)
    logits = logit_scale * similar + offset
    signed = labels * logits
    loss_sum = jnp.sum(jax.nn.softplus(-signed))
    slopes = (-labels * jax.nn.sigmoid(-signed) * logit_scale).astype(jnp.bfloat16)
    return (slopes, loss_sum)


def masked_tile(active_flag, image_side, text_side, labels, logit_scale, offset):

    def active(unused):
        return score_tile(image_side, text_side, labels, logit_scale, offset)

    def skipped(unused):
        return (
            jnp.zeros((image_side.shape[0], text_side.shape[0]), jnp.bfloat16),
            jnp.zeros((), jnp.float32),
        )

    return lax.cond(active_flag > 0, active, skipped, 0)


def body(image_emb, text_emb, positives, pair_mask, log_scale, bias):
    reach = (pair_mask.shape[1] - 1) // 2
    block_count = lax.axis_size("blk")
    myself = lax.axis_index("blk")
    logit_scale = jnp.exp(log_scale[0])
    offset = bias[0]
    row_count = image_emb.shape[0]
    image_normed, image_len = unit_rows(image_emb)
    text_normed, text_len = unit_rows(text_emb)
    image_half = image_normed.astype(jnp.bfloat16)
    text_half = text_normed.astype(jnp.bfloat16)
    columns = lax.broadcasted_iota(jnp.int32, (row_count, row_count), 1)
    own_labels = jnp.where(positives[0][:, None] == columns, 1.0, -1.0).astype(jnp.float32)
    apart_labels = -jnp.ones((row_count, row_count), jnp.float32)
    own_flags = lax.dynamic_index_in_dim(pair_mask, myself, 0, keepdims=False)
    fetched = {}
    for direction in (1, -1):
        moving = text_half
        for distance in range(1, reach + 1):
            moving = passed_along(moving, "blk", -direction)
            fetched[direction * distance] = moving
    slopes, loss_sum = masked_tile(
        own_flags[reach], image_half, text_half, own_labels, logit_scale, offset
    )
    image_total = jnp.dot(slopes, text_half, preferred_element_type=jnp.float32)
    text_total = jnp.einsum("rc,rd->cd", slopes, image_half, preferred_element_type=jnp.float32)
    for distance in range(-reach, reach + 1):
        if distance == 0:
            continue
        partner = fetched[distance]
        slopes, part_loss = masked_tile(
            own_flags[reach + distance], image_half, partner, apart_labels, logit_scale, offset
        )
        loss_sum = loss_sum + part_loss
        image_total = image_total + jnp.dot(slopes, partner, preferred_element_type=jnp.float32)
        partial_grad = jnp.einsum(
            "rc,rd->cd", slopes, image_half, preferred_element_type=jnp.float32
        ).astype(jnp.bfloat16)
        arrived = passed_along(partial_grad, "blk", distance)
        text_total = text_total + arrived.astype(jnp.float32)
    total_loss = lax.psum(loss_sum, ("blk", "grp"))
    image_count = row_count * block_count * lax.axis_size("grp")
    loss = (total_loss / image_count).reshape(1)
    image_grad = back_rows(image_normed, image_len, image_total).astype(jnp.bfloat16)
    text_grad = back_rows(text_normed, text_len, text_total).astype(jnp.bfloat16)
    return (image_grad, text_grad, loss)


def solution(mesh):
    return jax.shard_map(
        body,
        mesh=mesh,
        in_specs=(
            P(("blk", "grp"), None),
            P(("blk", "grp"), None),
            P(("blk", "grp"), None),
            P(),
            P(),
            P(),
        ),
        out_specs=(P(("blk", "grp"), None), P(("blk", "grp"), None), P()),
        check_vma=False,
    )
```

profile of v0, /device:TPU:0, one launch (start us, length us, event | category | flops | bytes accessed | tf_op | source)
XLA Modules:
  0.0 280.1 jit_solution(2164788945262324874)
XLA Ops:
  4.5 6.0 %collective-permute-start.3 = (bf16[384,1152]{1,0:T(8,128)(2,1)}, bf16[384,1152]{1,0:T(8,128)(2,1)}, u32[]{:S(2)}, u32[]{:S(2)}) collective-permute-start(bf16[384,1152]{1,0:T(8,128)(2,1)} %fusion.29), channel_id=1, source_target_pairs={{0,28},{4,0},{8,4},{12,8},{16,12},{20,16},{24,20},{28,24},{1,29},{... | collective-permute-start | bytes 2654216 | tf_op jit(solution)/shard_map/ppermute | solution.py:12
  13.2 4.2 %conditional.7 = (bf16[384,384]{1,0:T(8,128)(2,1)S(1)}, f32[]{:T(128)}) conditional(s32[]{:T(128)} %bitcast, () %tuple.71, (s32[1,384]{1,0:T(1,128)S(1)}, s32[384,384]{1,0:T(8,128)S(1)}, f32[]{:T(128)}, bf16[384,1152]{1,0:T(8,128)(2,1)S(1)}, bf16[384,1152]{1,0:T(8,128)(2,1)}, /*index=5*/f32[]{:T(128)}) %tuple.115), branch_computations={%region_2.3_spmd, %region_3.5_spmd} | conditional | flops 342540288 | bytes 2658848 | solution.py:46
  13.2 3.6 %fusion.23 = (f32[]{:T(128)}, bf16[384,384]{1,0:T(8,128)(2,1)S(1)}) fusion(f32[]{:T(128)} %get-tuple-element.82, f32[]{:T(128)} %get-tuple-element.85, bf16[384,1152]{1,0:T(8,128)(2,1)S(1)} %get-tuple-element.83, bf16[384,1152]{1,0:T(8,128)(2,1)} %get-tuple-element.84, s32[384,384]{1,0:T(8,128)S(1)} %get-tuple-element.81, s32[384]{0:T(512)S(1)} %reduce), kind=kOutput, calls=%fused_computation.44 | convolution fusion | flops 342540288 | bytes 2655756 | tf_op jit(solution)/shard_map/cond/branch_1_fun/rd,cd->rc/dot_general | solution.py:27
  17.4 29.2 %collective-permute-done = bf16[384,1152]{1,0:T(8,128)(2,1)} collective-permute-done((bf16[384,1152]{1,0:T(8,128)(2,1)}, bf16[384,1152]{1,0:T(8,128)(2,1)}, u32[]{:S(2)}, u32[]{:S(2)}) %collective-permute-start) | collective-permute-done | bytes 884768 | tf_op jit(solution)/shard_map/ppermute | solution.py:12
  59.1 4.2 %conditional.11 = (bf16[384,384]{1,0:T(8,128)(2,1)S(1)}, f32[]{:T(128)}) conditional(s32[]{:T(128)} %bitcast.6, () %tuple.79, (f32[]{:T(128)}, bf16[384,1152]{1,0:T(8,128)(2,1)S(1)}, bf16[384,1152]{1,0:T(8,128)(2,1)}, f32[]{:T(128)}) %tuple.80), branch_computations={%region_14.15_spmd, %region_15.17_spmd} | conditional | flops 341950464 | bytes 2064412 | solution.py:46
  59.2 3.5 %fusion.11 = (f32[]{:T(128)}, bf16[384,384]{1,0:T(8,128)(2,1)S(1)}) fusion(f32[]{:T(128)} %get-tuple-element.98, f32[]{:T(128)} %get-tuple-element.101, bf16[384,1152]{1,0:T(8,128)(2,1)S(1)} %get-tuple-element.99, bf16[384,1152]{1,0:T(8,128)(2,1)} %get-tuple-element.100), kind=kOutput, calls=%fused_computation.22 | convolution fusion | flops 341950464 | bytes 2064396 | tf_op jit(solution)/shard_map/cond/branch_1_fun/rd,cd->rc/dot_general | solution.py:27
  69.0 4.7 %collective-permute-start.8 = (bf16[384,1152]{1,0:T(8,128)(2,1)}, bf16[384,1152]{1,0:T(8,128)(2,1)}, u32[]{:S(2)}, u32[]{:S(2)}) collective-permute-start(bf16[384,1152]{1,0:T(8,128)(2,1)} %convolution_convert_fusion.3), channel_id=1, source_target_pairs={{0,28},{4,0},{8,4},{12,8},{16,12},{20,16},{24,20},{28,24},{1,29},{... | collective-permute-start | bytes 2654216 | tf_op jit(solution)/shard_map/ppermute | solution.py:12
  73.7 33.6 %collective-permute-done.1 = bf16[384,1152]{1,0:T(8,128)(2,1)} collective-permute-done((bf16[384,1152]{1,0:T(8,128)(2,1)}, bf16[384,1152]{1,0:T(8,128)(2,1)}, u32[]{:S(2)}, u32[]{:S(2)}) %collective-permute-start.1) | collective-permute-done | bytes 884768 | tf_op jit(solution)/shard_map/ppermute | solution.py:12
  109.8 3.0 %fusion.33 = f32[384,1152]{1,0:T(8,128)} fusion(bf16[384,384]{1,0:T(8,128)(2,1)S(1)} %copy-done.8, bf16[384,1152]{1,0:T(8,128)(2,1)} %collective-permute-done.3), kind=kOutput, calls=%fused_computation.77 | convolution fusion | flops 339738624 | bytes 2949120 | tf_op jit(solution)/shard_map/dot_general | solution.py:83
  115.2 3.1 %fusion.32 = f32[384,1152]{1,0:T(8,128)} fusion(bf16[384,384]{1,0:T(8,128)(2,1)} %get-tuple-element.130, bf16[384,1152]{1,0:T(8,128)(2,1)} %collective-permute-done), kind=kOutput, calls=%fused_computation.76 | convolution fusion | flops 339738624 | bytes 2949120 | tf_op jit(solution)/shard_map/dot_general | solution.py:83
  118.4 4.2 %conditional.12 = (bf16[384,384]{1,0:T(8,128)(2,1)S(1)}, f32[]{:T(128)}) conditional(s32[]{:T(128)} %bitcast.7, () %tuple.81, (f32[]{:T(128)}, bf16[384,1152]{1,0:T(8,128)(2,1)S(1)}, bf16[384,1152]{1,0:T(8,128)(2,1)}, f32[]{:T(128)}) %tuple.82), branch_computations={%region_17.18_spmd, %region_18.20_spmd} | conditional | flops 341950464 | bytes 2064412 | solution.py:46
  118.4 3.6 %fusion.14 = (f32[]{:T(128)}, bf16[384,384]{1,0:T(8,128)(2,1)S(1)}) fusion(f32[]{:T(128)} %get-tuple-element.102, f32[]{:T(128)} %get-tuple-element.105, bf16[384,1152]{1,0:T(8,128)(2,1)S(1)} %get-tuple-element.103, bf16[384,1152]{1,0:T(8,128)(2,1)} %get-tuple-element.104), kind=kOutput, calls=%fused_computation.28 | convolution fusion | flops 341950464 | bytes 2064396 | tf_op jit(solution)/shard_map/cond/branch_1_fun/rd,cd->rc/dot_general | solution.py:27
  124.9 4.9 %conditional.9 = (bf16[384,384]{1,0:T(8,128)(2,1)}, f32[]{:T(128)}) conditional(s32[]{:T(128)} %bitcast.4, () %tuple.75, (f32[]{:T(128)}, bf16[384,1152]{1,0:T(8,128)(2,1)S(1)}, bf16[384,1152]{1,0:T(8,128)(2,1)}, f32[]{:T(128)}) %tuple.76), branch_computations={%region_8.9_spmd, %region_9.11_spmd} | conditional | flops 341950464 | bytes 2064412 | solution.py:46
  124.9 4.2 %fusion.5 = (f32[]{:T(128)}, bf16[384,384]{1,0:T(8,128)(2,1)}) fusion(f32[]{:T(128)} %get-tuple-element.90, f32[]{:T(128)} %get-tuple-element.93, bf16[384,1152]{1,0:T(8,128)(2,1)S(1)} %get-tuple-element.91, bf16[384,1152]{1,0:T(8,128)(2,1)} %get-tuple-element.92), kind=kOutput, calls=%fused_computation.10 | convolution fusion | flops 341950464 | bytes 2064396 | tf_op jit(solution)/shard_map/cond/branch_1_fun/rd,cd->rc/dot_general | solution.py:27
  132.4 30.9 %collective-permute-done.2 = bf16[384,1152]{1,0:T(8,128)(2,1)} collective-permute-done((bf16[384,1152]{1,0:T(8,128)(2,1)}, bf16[384,1152]{1,0:T(8,128)(2,1)}, u32[]{:S(2)}, u32[]{:S(2)}) %collective-permute-start.2) | collective-permute-done | bytes 884768 | tf_op jit(solution)/shard_map/ppermute | solution.py:12
  167.4 4.9 %conditional.13 = (bf16[384,384]{1,0:T(8,128)(2,1)}, f32[]{:T(128)}) conditional(s32[]{:T(128)} %bitcast.8, () %tuple.83, (f32[]{:T(128)}, bf16[384,1152]{1,0:T(8,128)(2,1)S(1)}, bf16[384,1152]{1,0:T(8,128)(2,1)}, f32[]{:T(128)}) %tuple.84), branch_computations={%region_20.21_spmd, %region_21.23_spmd} | conditional | flops 341950464 | bytes 2064412 | solution.py:46
  167.4 4.2 %fusion.17 = (f32[]{:T(128)}, bf16[384,384]{1,0:T(8,128)(2,1)}) fusion(f32[]{:T(128)} %get-tuple-element.106, f32[]{:T(128)} %get-tuple-element.109, bf16[384,1152]{1,0:T(8,128)(2,1)S(1)} %get-tuple-element.107, bf16[384,1152]{1,0:T(8,128)(2,1)} %get-tuple-element.108), kind=kOutput, calls=%fused_computation.34 | convolution fusion | flops 341950464 | bytes 2064396 | tf_op jit(solution)/shard_map/cond/branch_1_fun/rd,cd->rc/dot_general | solution.py:27
  172.4 3.2 %convolution_add_fusion.3 = f32[384,1152]{1,0:T(8,128)} fusion(f32[384,1152]{1,0:T(8,128)S(1)} %fusion.31, bf16[384,384]{1,0:T(8,128)(2,1)} %copy-done.11, bf16[384,1152]{1,0:T(8,128)(2,1)} %collective-permute-done.2), kind=kOutput, calls=%fused_computation.51 | convolution fusion | flops 340180992 | bytes 4718592 | tf_op jit(solution)/shard_map/dot_general | solution.py:83
  175.5 2.7 convolution_convert_fusion
  180.5 3.2 %fusion.25 = f32[384,1152]{1,0:T(8,128)S(1)} fusion(f32[384,1152]{1,0:T(8,128)} %fusion.33, f32[384,1152]{1,0:T(8,128)} %fusion.32, f32[384,1152]{1,0:T(8,128)S(1)} %copy-done.3, bf16[384,384]{1,0:T(8,128)(2,1)} %get-tuple-element.129, bf16[384,1152]{1,0:T(8,128)(2,1)} %collective-permute-done.1), kind=kOutput, calls=%fused_computation.50 | convolution fusion | flops 341065728 | bytes 8257536 | tf_op jit(solution)/shard_map/dot_general | solution.py:83
  187.1 3.2 %multiply_reduce_fusion.1 = (f32[384]{0:T(512)S(1)}, f32[384,1152]{1,0:T(8,128)}) fusion(f32[384]{0:T(512)S(1)} %add_sqrt_fusion.1, bf16[384,1152]{1,0:T(8,128)(2,1)S(1)} %copy-done.2, f32[384,1152]{1,0:T(8,128)S(1)} %convolution_add_fusion.1, bf16[384,384]{1,0:T(8,128)(2,1)} %get-tuple-element.133, bf16[384,1152]{1,0:T(8,128)(2,1)} %collective-permute-done.5), kind=kOutput, calls=%fused_computation.68 | convolution fusion | flops 341950080 | bytes 5606400 | tf_op jit(solution)/shard_map/dot_general | solution.py:83
  190.3 80.1 %psum.7 = f32[]{:T(128)} all-reduce(f32[]{:T(128)S(6)} %add.185), channel_id=1, replica_groups=mesh['blk'=8,'grp'=4] {'blk','grp'}, use_global_device_ids=true, to_apply=%region_25.26 | all-reduce | flops 1 | bytes 8 | tf_op jit(solution)/shard_map/psum | solution.py:89
  271.1 2.9 %divide_convert_fusion.1 = bf16[384,1152]{1,0:T(8,128)(2,1)} fusion(f32[384,1152]{1,0:T(8,128)} %get-tuple-element.167, f32[384]{0:T(512)S(1)} %get-tuple-element.166, f32[384]{0:T(512)S(1)} %add_sqrt_fusion.1, bf16[384,1152]{1,0:T(8,128)(2,1)S(1)} %copy-done.2), kind=kLoop, calls=%fused_computation.67 | loop fusion | flops 2654208 | bytes 3542016 | tf_op jit(solution)/shard_map/convert_element_type | solution.py:92
  274.1 3.6 %multiply_reduce_fusion = (f32[384]{0:T(512)S(1)}, f32[384,1152]{1,0:T(8,128)S(1)}) fusion(f32[384]{0:T(512)S(1)} %add_sqrt_fusion, bf16[384,1152]{1,0:T(8,128)(2,1)S(1)} %copy-done.1, bf16[384,1152]{1,0:T(8,128)(2,1)} %collective-permute-done.11, bf16[384,1152]{1,0:T(8,128)(2,1)} %collective-permute-done.10, bf16[384,1152]{1,0:T(8,128)(2,1)} %collective-permute-done.9, ...), kind=kLoop, calls=%fused_computation.65 | loop fusion | flops 7077504 | bytes 9735168 | tf_op jit(solution)/shard_map/reduce_sum | solution.py:22
  (68 shorter events, 41.2 us)
Async XLA Ops:
  0.6 10.2 %copy-start = (s32[8,7]{1,0:T(8,128)S(1)}, s32[8,7]{1,0:T(8,128)}, u32[]{:S(2)}) copy-start(s32[8,7]{1,0:T(8,128)} %param.23) | copy-start | bytes 676
  0.6 9.9 %copy-start.2 = (bf16[384,1152]{1,0:T(8,128)(2,1)S(1)}, bf16[384,1152]{1,0:T(8,128)(2,1)}, u32[]{:S(2)}) copy-start(bf16[384,1152]{1,0:T(8,128)(2,1)} %param.20) | copy-start | bytes 2654212
  4.5 8.7 %copy-start.12 = (s32[1,384]{1,0:T(1,128)S(1)}, s32[1,384]{1,0:T(1,128)}, u32[]{:S(2)}) copy-start(s32[1,384]{1,0:T(1,128)} %param.22) | copy-start | bytes 4612
  4.5 46.5 %collective-permute-start.3 = (bf16[384,1152]{1,0:T(8,128)(2,1)}, bf16[384,1152]{1,0:T(8,128)(2,1)}, u32[]{:S(2)}, u32[]{:S(2)}) collective-permute-start(bf16[384,1152]{1,0:T(8,128)(2,1)} %fusion.29), channel_id=1, source_target_pairs={{0,28},{4,0},{8,4},{12,8},{16,12},{20,16},{24,20},{28,24},{1,29},{... | collective-permute-start | bytes 2654216 | tf_op jit(solution)/shard_map/ppermute | solution.py:12
  10.6 36.0 %collective-permute-start = (bf16[384,1152]{1,0:T(8,128)(2,1)}, bf16[384,1152]{1,0:T(8,128)(2,1)}, u32[]{:S(2)}, u32[]{:S(2)}) collective-permute-start(bf16[384,1152]{1,0:T(8,128)(2,1)} %fusion.29), channel_id=1, source_target_pairs={{0,4},{4,8},{8,12},{12,16},{16,20},{20,24},{24,28},{28,0},{1,5},{5... | collective-permute-start | bytes 2654216 | tf_op jit(solution)/shard_map/ppermute | solution.py:12
  17.4 31.6 %copy-start.5 = (bf16[384,384]{1,0:T(8,128)(2,1)}, bf16[384,384]{1,0:T(8,128)(2,1)S(1)}, u32[]{:S(2)}) copy-start(bf16[384,384]{1,0:T(8,128)(2,1)S(1)} %get-tuple-element.127) | copy-start | bytes 884740
  46.6 60.8 %collective-permute-start.1 = (bf16[384,1152]{1,0:T(8,128)(2,1)}, bf16[384,1152]{1,0:T(8,128)(2,1)}, u32[]{:S(2)}, u32[]{:S(2)}) collective-permute-start(bf16[384,1152]{1,0:T(8,128)(2,1)} %collective-permute-done), channel_id=1, source_target_pairs={{0,4},{4,8},{8,12},{12,16},{16,20},{20,24},{24,28},{28,0},{1,5},{5... | collective-permute-start | bytes 2654216 | tf_op jit(solution)/shard_map/ppermute | solution.py:12
  49.1 4.4 %copy-start.6 = (bf16[384,384]{1,0:T(8,128)(2,1)S(1)}, bf16[384,384]{1,0:T(8,128)(2,1)}, u32[]{:S(2)}) copy-start(bf16[384,384]{1,0:T(8,128)(2,1)} %copy-done.5) | copy-start | bytes 884740
  51.0 61.8 %collective-permute-start.4 = (bf16[384,1152]{1,0:T(8,128)(2,1)}, bf16[384,1152]{1,0:T(8,128)(2,1)}, u32[]{:S(2)}, u32[]{:S(2)}) collective-permute-start(bf16[384,1152]{1,0:T(8,128)(2,1)} %collective-permute-done.3), channel_id=1, source_target_pairs={{0,28},{4,0},{8,4},{12,8},{16,12},{20,16},{24,20},{28,24},{1,29},{... | collective-permute-start | bytes 2654216 | tf_op jit(solution)/shard_map/ppermute | solution.py:12
  63.4 0.7 copy-start.7
  65.7 119.8 %collective-permute-start.9 = (bf16[384,1152]{1,0:T(8,128)(2,1)}, bf16[384,1152]{1,0:T(8,128)(2,1)}, u32[]{:S(2)}, u32[]{:S(2)}) collective-permute-start(bf16[384,1152]{1,0:T(8,128)(2,1)} %convolution_convert_fusion.2), channel_id=1, source_target_pairs={{0,4},{4,8},{8,12},{12,16},{16,20},{20,24},{24,28},{28,0},{1,5},{5... | collective-permute-start | bytes 2654216 | tf_op jit(solution)/shard_map/ppermute | solution.py:12
  66.4 43.4 %copy-start.8 = (bf16[384,384]{1,0:T(8,128)(2,1)S(1)}, bf16[384,384]{1,0:T(8,128)(2,1)}, u32[]{:S(2)}) copy-start(bf16[384,384]{1,0:T(8,128)(2,1)} %copy-done.7) | copy-start | bytes 884740
  69.0 205.0 %collective-permute-start.8 = (bf16[384,1152]{1,0:T(8,128)(2,1)}, bf16[384,1152]{1,0:T(8,128)(2,1)}, u32[]{:S(2)}, u32[]{:S(2)}) collective-permute-start(bf16[384,1152]{1,0:T(8,128)(2,1)} %convolution_convert_fusion.3), channel_id=1, source_target_pairs={{0,28},{4,0},{8,4},{12,8},{16,12},{20,16},{24,20},{28,24},{1,29},{... | collective-permute-start | bytes 2654216 | tf_op jit(solution)/shard_map/ppermute | solution.py:12
  107.4 55.9 %collective-permute-start.2 = (bf16[384,1152]{1,0:T(8,128)(2,1)}, bf16[384,1152]{1,0:T(8,128)(2,1)}, u32[]{:S(2)}, u32[]{:S(2)}) collective-permute-start(bf16[384,1152]{1,0:T(8,128)(2,1)} %collective-permute-done.1), channel_id=1, source_target_pairs={{0,4},{4,8},{8,12},{12,16},{16,20},{20,24},{24,28},{28,0},{1,5},{5... | collective-permute-start | bytes 2654216 | tf_op jit(solution)/shard_map/ppermute | solution.py:12
  112.9 54.6 %collective-permute-start.5 = (bf16[384,1152]{1,0:T(8,128)(2,1)}, bf16[384,1152]{1,0:T(8,128)(2,1)}, u32[]{:S(2)}, u32[]{:S(2)}) collective-permute-start(bf16[384,1152]{1,0:T(8,128)(2,1)} %collective-permute-done.4), channel_id=1, source_target_pairs={{0,28},{4,0},{8,4},{12,8},{16,12},{20,16},{24,20},{28,24},{1,29},{... | collective-permute-start | bytes 2654216 | tf_op jit(solution)/shard_map/ppermute | solution.py:12
  124.9 149.2 %collective-permute-start.10 = (bf16[384,1152]{1,0:T(8,128)(2,1)}, bf16[384,1152]{1,0:T(8,128)(2,1)}, u32[]{:S(2)}, u32[]{:S(2)}) collective-permute-start(bf16[384,1152]{1,0:T(8,128)(2,1)} %convolution_convert_fusion.1), channel_id=1, source_target_pairs={{0,8},{4,12},{8,16},{12,20},{16,24},{20,28},{24,0},{28,4},{1,9},{5... | collective-permute-start | bytes 2654216 | tf_op jit(solution)/shard_map/ppermute | solution.py:12
  163.3 110.8 %collective-permute-start.7 = (bf16[384,1152]{1,0:T(8,128)(2,1)}, bf16[384,1152]{1,0:T(8,128)(2,1)}, u32[]{:S(2)}, u32[]{:S(2)}) collective-permute-start(bf16[384,1152]{1,0:T(8,128)(2,1)} %convolution_convert_fusion.4), channel_id=1, source_target_pairs={{0,24},{4,28},{8,0},{12,4},{16,8},{20,12},{24,16},{28,20},{1,25},{... | collective-permute-start | bytes 2654216 | tf_op jit(solution)/shard_map/ppermute | solution.py:12
  165.1 0.7 copy-start.11
  175.5 4.9 %copy-start.3 = (f32[384,1152]{1,0:T(8,128)S(1)}, f32[384,1152]{1,0:T(8,128)}, u32[]{:S(2)}) copy-start(f32[384,1152]{1,0:T(8,128)} %convolution_add_fusion.3) | copy-start | bytes 5308420
  178.2 95.9 %collective-permute-start.11 = (bf16[384,1152]{1,0:T(8,128)(2,1)}, bf16[384,1152]{1,0:T(8,128)(2,1)}, u32[]{:S(2)}, u32[]{:S(2)}) collective-permute-start(bf16[384,1152]{1,0:T(8,128)(2,1)} %convolution_convert_fusion), channel_id=1, source_target_pairs={{0,12},{4,16},{8,20},{12,24},{16,28},{20,0},{24,4},{28,8},{1,13},{... | collective-permute-start | bytes 2654216 | tf_op jit(solution)/shard_map/ppermute | solution.py:12
  180.5 3.2 %copy-start.10 = (bf16[384,384]{1,0:T(8,128)(2,1)S(1)}, bf16[384,384]{1,0:T(8,128)(2,1)}, u32[]{:S(2)}) copy-start(bf16[384,384]{1,0:T(8,128)(2,1)} %copy-done.9) | copy-start | bytes 884740
  185.5 88.6 %collective-permute-start.6 = (bf16[384,1152]{1,0:T(8,128)(2,1)}, bf16[384,1152]{1,0:T(8,128)(2,1)}, u32[]{:S(2)}, u32[]{:S(2)}) collective-permute-start(bf16[384,1152]{1,0:T(8,128)(2,1)} %convolution_convert_fusion.5), channel_id=1, source_target_pairs={{0,20},{4,24},{8,28},{12,0},{16,4},{20,8},{24,12},{28,16},{1,21},{... | collective-permute-start | bytes 2654216 | tf_op jit(solution)/shard_map/ppermute | solution.py:12
  271.1 3.0 %copy-start.1 = (bf16[384,1152]{1,0:T(8,128)(2,1)S(1)}, bf16[384,1152]{1,0:T(8,128)(2,1)}, u32[]{:S(2)}) copy-start(bf16[384,1152]{1,0:T(8,128)(2,1)} %param.21) | copy-start | bytes 2654212
  271.1 3.0 %copy-start.4 = (f32[384,1152]{1,0:T(8,128)S(1)}, f32[384,1152]{1,0:T(8,128)}, u32[]{:S(2)}) copy-start(f32[384,1152]{1,0:T(8,128)} %fusion.34) | copy-start | bytes 5308420
  (1 other events, 0.7 us)
where the time goes:
time: 281 us; the launch traced here: 280 us
  waiting for transfers between devices  93.7 us (33%)
  blocking collectives  80.1 us (29%)
  matrix products  53.2 us (19%)
  starting transfers between devices  26 us (9%)
  other arithmetic  12.2 us (4%)
  between operations  7.79 us (3%)
  local copies, waits for them, and re-layouts  3.65 us (1%)
  loops' own time  3.43 us (1%)
    ppermute x12, waiting for transfers between devices, passed_along(): return lax.ppermute(value, axis, pairs)  93.7 us
    psum x1, blocking collectives, body(): total_loss = lax.psum(loss_sum, ('blk', 'grp'))  80.1 us
    ppermute x12, starting transfers between devices, passed_along(): return lax.ppermute(value, axis, pairs)  26 us
    dot_general x5, matrix products, score_tile(): jnp.einsum('rd,cd->rc', image_side, text_side, preferred_element_type=jnp...  19.2 us
    dot_general x6, matrix products, body(): jnp.dot(slopes, partner, preferred_element_type=jnp.float32)  17.5 us
    dot_general x7, matrix products, body(): jnp.einsum('rc,rd->cd', slopes, image_half, preferred_element_type=jnp.fl...  14.5 us
  transfers between devices with their start and end apart: 12, of which 3 were waited for; matrix products, arithmetic and copies ran while one was open for 21% of the time, Pallas kernels for 0%

commit v1 on v0

--- a/solution.py
+++ b/solution.py
@@ -1,6 +1,10 @@
+import functools
+
 import jax
 import jax.numpy as jnp
 from jax import lax
+from jax.experimental import pallas as pl
+from jax.experimental.pallas import tpu as pltpu
 from jax.sharding import PartitionSpec as P
 
 epsilon = 1e-06
@@ -46,7 +50,7 @@
     return lax.cond(active_flag > 0, active, skipped, 0)
 
 
-def body(image_emb, text_emb, positives, pair_mask, log_scale, bias):
+def plain_body(image_emb, text_emb, positives, pair_mask, log_scale, bias):
     reach = (pair_mask.shape[1] - 1) // 2
     block_count = lax.axis_size("blk")
     myself = lax.axis_index("blk")
@@ -94,6 +98,284 @@
     return (image_grad, text_grad, loss)
 
 
+MESH = pl.DeviceIdType.MESH
+Y, INNER, OUTER = 0, 1, 2
+
+
+def grid_kernel(reach, parts, mask_ref, scale_ref, offset_ref, image_ref, text_ref, pos_row, pos_col,
+                image_out, text_out, loss_out,
+                got, own, tmp, acc, loss_acc, send_sem, recv_sem):
+    me = lax.axis_index("blk")
+    grp = lax.axis_index("grp")
+    count = lax.axis_size("blk")
+    rows = image_ref.shape[0]
+    piece = rows // parts
+    row, col = me // 2, me % 2
+    top = row // 2
+    role = row + top * (3 - 2 * row)
+    toward = 1 - 2 * top
+    aside = row * 2 + (1 - col)
+    inner = (row + toward) * 2 + col
+    outer = lax.rem((row - toward + 4), 4) * 2 + col
+    targets = {Y: aside, INNER: inner, OUTER: outer}
+    is_end, is_mid = role == 0, role == 1
+    raw = (text_ref, image_ref)
+
+    def block(p, c):
+        place = p + top * (3 - 2 * p)
+        return place * 2 + col + c * (1 - 2 * col)
+
+    def cut(c):
+        return pl.ds(pl.multiple_of(c * piece, piece), piece)
+
+    def remote(way, slot, source, kind, which, c):
+        return pltpu.make_async_remote_copy(
+            src_ref=source.at[cut(c)], dst_ref=got.at[kind, which, cut(c)],
+            send_sem=send_sem.at[way, slot, kind, c], recv_sem=recv_sem.at[kind, which, c],
+            device_id=(targets[way], grp), device_id_type=MESH)
+
+    def forward(way, slot, kind, which, c):
+        remote(way, slot, got.at[kind, which], kind, which, c).start()
+
+    def arrived(kind, which, c):
+        remote(Y, 0, got.at[kind, which], kind, which, c).wait_recv()
+
+    barrier = pltpu.get_barrier_semaphore()
+    pl.semaphore_signal(barrier, inc=1, device_id=(aside, grp), device_id_type=MESH)
+    pl.semaphore_signal(barrier, inc=1, device_id=(inner, grp), device_id_type=MESH)
+
+    @pl.when(is_mid)
+    def _():
+        pl.semaphore_signal(barrier, inc=1, device_id=(outer, grp), device_id_type=MESH)
+        pl.semaphore_wait(barrier, 3)
+
+    @pl.when(is_end)
+    def _():
+        pl.semaphore_wait(barrier, 2)
+
+    for kind in (0, 1):
+        @pl.loop(0, parts)
+        def _(c, kind=kind):
+            remote(Y, 0, raw[kind], kind, me, c).start()
+            remote(INNER, 0, raw[kind], kind, me, c).start()
+
+            @pl.when(is_mid)
+            def _():
+                remote(OUTER, 0, raw[kind], kind, me, c).start()
+
+    scale = jnp.exp(scale_ref[...])
+    offset = offset_ref[...]
+
+    def normalise(source, target):
+        @pl.loop(0, parts)
+        def _(c):
+            values = source[cut(c), :].astype(jnp.float32)
+            length = jnp.sqrt(jnp.sum(values * values, axis=1, keepdims=True) + epsilon)
+            target[cut(c), :] = (values / length).astype(jnp.bfloat16)
+
+    def tile(c, side, other):
+        similar = lax.dot_general(own[side, cut(c), :], other[...], (((1,), (1,)), ((), ())),
+                                  preferred_element_type=jnp.float32)
+        return scale * similar + offset
+
+    def flag_of(side, which):
+        if side == 0:
+            apart = lax.rem(which - me + reach + count, count)
+            return mask_ref[me, apart].astype(jnp.float32)
+        apart = lax.rem(me - which + reach + count, count)
+        return mask_ref[which, apart].astype(jnp.float32)
+
+    def item(side, which):
+        normalise(got.at[side, which], tmp)
+        flag = flag_of(side, which)
+
+        @pl.loop(0, parts)
+        def _(c):
+            grown = jnp.exp(tile(c, side, tmp))
+            slopes = (grown / (1.0 + grown) * (scale * flag)).astype(jnp.bfloat16)
+            acc[side, cut(c), :] += jnp.dot(slopes, tmp[...], preferred_element_type=jnp.float32)
+            if side == 0:
+                loss_acc[...] += flag * jnp.sum(jnp.log1p(grown), axis=0, keepdims=True)
+
+    def own_item(side):
+        @pl.loop(0, parts)
+        def _(c):
+            logits = tile(c, side, own.at[1 - side])
+            flag = mask_ref[me, reach].astype(jnp.float32)
+            if side == 0:
+                match = pos_col[cut(c), :] == lax.broadcasted_iota(jnp.int32, logits.shape, 1)
+            else:
+                match = pos_row[...] == lax.broadcasted_iota(jnp.int32, logits.shape, 0) + c * piece
+            labels = jnp.where(match, 1.0, -1.0)
+            grown = jnp.exp(-labels * logits)
+            slopes = (-labels * grown / (1.0 + grown) * (scale * flag)).astype(jnp.bfloat16)
+            acc[side, cut(c), :] = jnp.dot(slopes, own[1 - side], preferred_element_type=jnp.float32)
+            if side == 0:
+                loss_acc[...] += flag * jnp.sum(jnp.log1p(grown), axis=0, keepdims=True)
+
+    loss_acc[...] = jnp.zeros_like(loss_acc)
+    normalise(image_ref, own.at[0])
+    normalise(text_ref, own.at[1])
+
+    steps = 2 * parts
+
+    @pl.loop(0, steps)
+    def _(step):
+        kind, c = step // parts, step % parts
+
+        @pl.when(is_mid)
+        def _():
+            arrived(kind, block(0, 0), c)
+            forward(INNER, 1, kind, block(0, 0), c)
+            forward(Y, 1, kind, block(0, 0), c)
+            arrived(kind, block(2, 0), c)
+            arrived(kind, block(1, 1), c)
+
+        @pl.when(is_end)
+        def _():
+            arrived(kind, block(1, 0), c)
+            forward(Y, 1, kind, block(1, 0), c)
+            arrived(kind, block(0, 1), c)
+
+        @pl.when(step == 0)
+        def _():
+            own_item(0)
+
+        @pl.when(step == 1)
+        def _():
+            own_item(1)
+
+    @pl.when(is_mid)
+    def _():
+        @pl.loop(0, steps)
+        def _(step):
+            forward(INNER, 2, step // parts, block(1, 1), step % parts)
+
+    def first_block(i):
+        mid_p, mid_c = (2 * i) * (2 - i) + i // 2, i // 2
+        end_p, end_c = 1 - i % 2, i % 2
+        return block(role * mid_p + (1 - role) * end_p, role * mid_c + (1 - role) * end_c)
+
+    @pl.loop(0, steps)
+    def _(step):
+        kind, c = step // parts, step % parts
+        arrived(kind, block(3, 0), c)
+        forward(Y, 2, kind, block(3, 0), c)
+
+        @pl.when(is_mid)
+        def _():
+            forward(OUTER, 1, kind, block(3, 0), c)
+
+        which = first_block(step // 2)
+
+        @pl.when(step % 2 + 0 * role == 0)
+        def _():
+            @pl.when(step < 4 + 2 * role)
+            def _():
+                item(0, which)
+
+        @pl.when(step % 2 == 1)
+        def _():
+            @pl.when(step < 4 + 2 * role)
+            def _():
+                item(1, which)
+
+        arrived(kind, block(1 - role, 1), c)
+
+    def second_block(i):
+        return block((1 - role) * (3 - 2 * i), (1 - role) * i + role)
+
+    @pl.loop(0, steps)
+    def _(step):
+        kind, c = step // parts, step % parts
+        arrived(kind, block(2, 1), c)
+
+        @pl.when(is_mid)
+        def _():
+            forward(OUTER, 2, kind, block(2, 1), c)
+
+        late = step // 4
+        which = (1 - late) * second_block(step // 2) + late * block(step - 2, 1)
+        busy = 1 - (1 - late) * role * (step // 2)
+
+        @pl.when(busy == 1)
+        def _():
+            @pl.when((1 - late) * (step % 2) == 0)
+            def _():
+                item(0, which)
+
+            @pl.when((1 - late) * (step % 2) == 1)
+            def _():
+                item(1, which)
+
+        arrived(kind, block(3, 1), c)
+
+    @pl.loop(2, 4)
+    def _(p):
+        item(1, block(p, 1))
+
+    for side, source, result in ((0, image_ref, image_out), (1, text_ref, text_out)):
+        @pl.loop(0, parts)
+        def _(c, side=side, source=source, result=result):
+            values = source[cut(c), :].astype(jnp.float32)
+            length = jnp.sqrt(jnp.sum(values * values, axis=1, keepdims=True) + epsilon)
+            normed = values / length
+            result[cut(c), :] = back_rows(normed, length, acc[side, cut(c), :]).astype(result.dtype)
+
+    loss_out[...] = loss_acc[...]
+
+    @pl.loop(0, steps)
+    def _(step):
+        kind, c = step // parts, step % parts
+        for slot in range(3):
+            remote(Y, slot, got.at[kind, me], kind, me, c).wait_send()
+
+        remote(INNER, 0, got.at[kind, me], kind, me, c).wait_send()
+
+        @pl.when(is_mid)
+        def _():
+            remote(INNER, 1, got.at[kind, me], kind, me, c).wait_send()
+            remote(INNER, 2, got.at[kind, me], kind, me, c).wait_send()
+            for slot in range(3):
+                remote(OUTER, slot, got.at[kind, me], kind, me, c).wait_send()
+
+
+def body(image_emb, text_emb, positives, pair_mask, log_scale, bias):
+    reach = (pair_mask.shape[1] - 1) // 2
+    block_count = lax.axis_size("blk")
+    row_count, width = image_emb.shape
+    if block_count != 2 * (reach + 1) or reach != 3 or row_count % (3 * 128) != 0:
+        return plain_body(image_emb, text_emb, positives, pair_mask, log_scale, bias)
+    parts = 3
+    vmem = pl.BlockSpec(memory_space=pltpu.VMEM)
+    image_grad, text_grad, losses = pl.pallas_call(
+        functools.partial(grid_kernel, reach, parts),
+        out_shape=(
+            jax.ShapeDtypeStruct(image_emb.shape, image_emb.dtype),
+            jax.ShapeDtypeStruct(text_emb.shape, text_emb.dtype),
+            jax.ShapeDtypeStruct((1, row_count), jnp.float32),
+        ),
+        in_specs=[pl.BlockSpec(memory_space=pltpu.SMEM)] + [vmem] * 6,
+        out_specs=(vmem,) * 3,
+        scratch_shapes=[
+            pltpu.VMEM((2, block_count, row_count, width), jnp.bfloat16),
+            pltpu.VMEM((2, row_count, width), jnp.bfloat16),
+            pltpu.VMEM((row_count, width), jnp.bfloat16),
+            pltpu.VMEM((2, row_count, width), jnp.float32),
+            pltpu.VMEM((1, row_count), jnp.float32),
+            pltpu.SemaphoreType.DMA((3, 3, 2, parts)),
+            pltpu.SemaphoreType.DMA((2, block_count, parts)),
+        ],
+        compiler_params=pltpu.CompilerParams(
+            collective_id=0, has_side_effects=True, vmem_limit_bytes=48 * 1024 * 1024
+        ),
+    )(pair_mask, log_scale.reshape(1, 1), bias.reshape(1, 1), image_emb, text_emb, positives,
+      positives.reshape(row_count, 1))
+    total_loss = lax.psum(jnp.sum(losses), ("blk", "grp"))
+    image_count = row_count * block_count * lax.axis_size("grp")
+    return (image_grad, text_grad, (total_loss / image_count).reshape(1))
+
+
 def solution(mesh):
     return jax.shard_map(
         body,

time: 281 us -> 188 us (0.67)
  Pallas kernels: 0 us -> 139 us
  waiting for transfers between devices: 93.7 us -> 0 us
  matrix products: 53.2 us -> 0 us
  blocking collectives: 80.1 us -> 38 us
  starting transfers between devices: 26 us -> 0 us
  other arithmetic: 12.2 us -> 0.6 us
  between operations: 7.79 us -> 3.74 us
  loops' own time: 3.43 us -> 0 us
    pallas_call x0 -> x1, Pallas kernels: none -> 139 us  [body(): pl.pallas_call(functools.partial(grid_kernel, reach, parts), out_shape=(j...]
    ppermute x12 -> x0, waiting for transfers between devices: 93.7 us -> none  [passed_along(): return lax.ppermute(value, axis, pairs)]
    dot_general x19 -> x0, matrix products: 53.2 us -> none  [the longest x5 19.2 us: score_tile(): jnp.einsum('rd,cd->rc', image_side, text_side, preferred_element_type=jnp...]
    psum x1, blocking collectives: 80.1 us -> 38 us  [body(): total_loss = lax.psum(jnp.sum(losses), ('blk', 'grp'))]
    ppermute x12 -> x0, starting transfers between devices: 26 us -> none  [passed_along(): return lax.ppermute(value, axis, pairs)]
    convert_element_type x4 -> x0, other arithmetic: 6.9 us -> none  [the longest x1 2.95 us: body(): back_rows(image_normed, image_len, image_total).astype(jnp.bfloat16)]
    reduce_sum x3 -> x1, other arithmetic: 5.3 us -> 0.6 us  [body(): total_loss = lax.psum(jnp.sum(losses), ('blk', 'grp'))]
    another operation x7 -> x0, loops' own time: 3.43 us -> none  [masked_tile(): return lax.cond(active_flag > 0, active, skipped, 0)]
  transfers between devices with their start and end apart: 12 -> 0, of which waited for: 3 -> 0; matrix products, arithmetic and copies ran while one was open for 21% -> 0% of each run, Pallas kernels for 0% -> 0%
where the time goes in v1:
time: 188 us; the launch traced here: 187 us
  Pallas kernels  139 us (74%)
  blocking collectives  38 us (20%)
  local copies, waits for them, and re-layouts  5.51 us (3%)
  between operations  3.74 us (2%)
    pallas_call x1, Pallas kernels, body(): pl.pallas_call(functools.partial(grid_kernel, reach, parts), out_shape=(j...  139 us
    psum x1, blocking collectives, body(): total_loss = lax.psum(jnp.sum(losses), ('blk', 'grp'))  38 us
    unnamed x10, local copies, waits for them, and re-layouts  5.38 us

profile of v1, /device:TPU:0, one launch (start us, length us, event | category | flops | bytes accessed | tf_op | source)
XLA Modules:
  0.0 186.6 jit_solution(15881368050017016785)
XLA Ops:
  1.9 0.0 copy-start.2
  1.9 0.7 copy-done.2
  2.6 0.0 copy-start.3
  2.6 0.1 copy.9.pos_col
  2.8 0.5 copy-done.3
  3.3 0.0 copy-start
  3.3 1.2 copy-done
  4.5 0.0 copy-start.1
  4.5 1.2 copy-done.1
  5.6 138.7 %shard_map.85 = (bf16[384,1152]{1,0:T(8,128)(2,1)S(1)}, bf16[384,1152]{1,0:T(8,128)(2,1)S(1)}, f32[1,384]{1,0:T(1,128)S(1)}) custom-call(s32[8,7]{1,0:T(8,128)S(1)} %copy-done.3, f32[1,1]{1,0:T(1,128)} %bitcast.4.scale_ref, f32[1,1]{1,0:T(1,128)} %bitcast.5.offset_ref, bf16[384,1152]{1,0:T(8,128)(2,1)S(1)} %copy-done, bf16[384,1152]{1,0:T(8,128)(2,1)S(1)} %copy-done.1, ...), custom_call_target="tpu_custom_call" | custom-call | tf_op jit(solution)/shard_map/pallas_call | solution.py:351
  144.4 0.6 reduce_sum.9
  145.0 38.0 %psum.7 = f32[]{:T(128)} all-reduce(f32[]{:T(128)} %reduce_sum.9), channel_id=1, replica_groups=mesh['blk'=8,'grp'=4] {'blk','grp'}, use_global_device_ids=true, to_apply=%region_1.0 | all-reduce | flops 1 | bytes 8 | tf_op jit(solution)/shard_map/psum | solution.py:374
  183.6 0.9 copy.14
  184.5 0.9 copy.15
Async XLA Ops:
  1.9 0.7 copy-start.2
  2.6 0.7 copy-start.3
  3.3 1.2 copy-start
  4.5 1.2 copy-start.1

commit v2 on v1

--- a/solution.py
+++ b/solution.py
@@ -102,14 +102,18 @@
 Y, INNER, OUTER = 0, 1, 2
 
 
-def grid_kernel(reach, parts, mask_ref, scale_ref, offset_ref, image_ref, text_ref, pos_row, pos_col,
+def grid_kernel(reach, parts, tiles, mask_ref, scale_ref, offset_ref, image_hbm, text_hbm, pos_row, pos_col,
                 image_out, text_out, loss_out,
-                got, own, tmp, acc, loss_acc, send_sem, recv_sem):
+                held, got, own, tmp, acc, loss_acc, blk_loss, grp_loss,
+                load_sem, send_sem, recv_sem, blk_send, blk_recv, grp_send, grp_recv):
     me = lax.axis_index("blk")
     grp = lax.axis_index("grp")
     count = lax.axis_size("blk")
-    rows = image_ref.shape[0]
+    groups = lax.axis_size("grp")
+    rows = held.shape[1]
     piece = rows // parts
+    tall = rows // tiles
+    image_ref, text_ref = held.at[1], held.at[0]
     row, col = me // 2, me % 2
     top = row // 2
     role = row + top * (3 - 2 * row)
@@ -128,6 +132,9 @@
     def cut(c):
         return pl.ds(pl.multiple_of(c * piece, piece), piece)
 
+    def band(c):
+        return pl.ds(pl.multiple_of(c * tall, tall), tall)
+
     def remote(way, slot, source, kind, which, c):
         return pltpu.make_async_remote_copy(
             src_ref=source.at[cut(c)], dst_ref=got.at[kind, which, cut(c)],
@@ -140,20 +147,51 @@
     def arrived(kind, which, c):
         remote(Y, 0, got.at[kind, which], kind, which, c).wait_recv()
 
+    loads = [
+        pltpu.make_async_copy(source, held.at[kind], load_sem.at[kind])
+        for kind, source in ((0, text_hbm), (1, image_hbm))
+    ]
+    for load in loads:
+        load.start()
     barrier = pltpu.get_barrier_semaphore()
-    pl.semaphore_signal(barrier, inc=1, device_id=(aside, grp), device_id_type=MESH)
-    pl.semaphore_signal(barrier, inc=1, device_id=(inner, grp), device_id_type=MESH)
-
-    @pl.when(is_mid)
-    def _():
-        pl.semaphore_signal(barrier, inc=1, device_id=(outer, grp), device_id_type=MESH)
-        pl.semaphore_wait(barrier, 3)
-
-    @pl.when(is_end)
-    def _():
-        pl.semaphore_wait(barrier, 2)
+
+    @pl.loop(1, count)
+    def _(d):
+        pl.semaphore_signal(barrier, inc=1, device_id=(lax.rem(me + d, count), grp), device_id_type=MESH)
+
+    @pl.loop(1, groups)
+    def _(d):
+        pl.semaphore_signal(barrier, inc=1, device_id=(me, lax.rem(grp + d, groups)), device_id_type=MESH)
+
+    pl.semaphore_wait(barrier, count + groups - 2)
+
+    def blk_share(d):
+        target = lax.rem(me + d, count)
+        return pltpu.make_async_remote_copy(
+            src_ref=blk_loss.at[me], dst_ref=blk_loss.at[me], send_sem=blk_send.at[d],
+            recv_sem=blk_recv.at[me], device_id=(target, grp), device_id_type=MESH)
+
+    def blk_arrival(d):
+        source = lax.rem(me + d, count)
+        return pltpu.make_async_remote_copy(
+            src_ref=blk_loss.at[source], dst_ref=blk_loss.at[source], send_sem=blk_send.at[d],
+            recv_sem=blk_recv.at[source], device_id=(source, grp), device_id_type=MESH)
+
+    def grp_share(d):
+        target = lax.rem(grp + d, groups)
+        return pltpu.make_async_remote_copy(
+            src_ref=grp_loss.at[grp], dst_ref=grp_loss.at[grp], send_sem=grp_send.at[d],
+            recv_sem=grp_recv.at[grp], device_id=(me, target), device_id_type=MESH)
+
+    def grp_arrival(d):
+        source = lax.rem(grp + d, groups)
+        return pltpu.make_async_remote_copy(
+            src_ref=grp_loss.at[source], dst_ref=grp_loss.at[source], send_sem=grp_send.at[d],
+            recv_sem=grp_recv.at[source], device_id=(me, source), device_id_type=MESH)
 
     for kind in (0, 1):
+        loads[kind].wait()
+
         @pl.loop(0, parts)
         def _(c, kind=kind):
             remote(Y, 0, raw[kind], kind, me, c).start()
@@ -163,18 +201,18 @@
             def _():
                 remote(OUTER, 0, raw[kind], kind, me, c).start()
 
-    scale = jnp.exp(scale_ref[...])
-    offset = offset_ref[...]
+    scale = jnp.exp(jnp.full((1, 1), scale_ref[0], jnp.float32))
+    offset = jnp.full((1, 1), offset_ref[0], jnp.float32)
 
     def normalise(source, target):
-        @pl.loop(0, parts)
+        @pl.loop(0, tiles)
         def _(c):
-            values = source[cut(c), :].astype(jnp.float32)
+            values = source[band(c), :].astype(jnp.float32)
             length = jnp.sqrt(jnp.sum(values * values, axis=1, keepdims=True) + epsilon)
-            target[cut(c), :] = (values / length).astype(jnp.bfloat16)
+            target[band(c), :] = (values / length).astype(jnp.bfloat16)
 
     def tile(c, side, other):
-        similar = lax.dot_general(own[side, cut(c), :], other[...], (((1,), (1,)), ((), ())),
+        similar = lax.dot_general(own[side, band(c), :], other[...], (((1,), (1,)), ((), ())),
                                   preferred_element_type=jnp.float32)
         return scale * similar + offset
 
@@ -189,29 +227,49 @@
         normalise(got.at[side, which], tmp)
         flag = flag_of(side, which)
 
-        @pl.loop(0, parts)
+        @pl.loop(0, tiles)
         def _(c):
             grown = jnp.exp(tile(c, side, tmp))
             slopes = (grown / (1.0 + grown) * (scale * flag)).astype(jnp.bfloat16)
-            acc[side, cut(c), :] += jnp.dot(slopes, tmp[...], preferred_element_type=jnp.float32)
+            acc[side, band(c), :] += jnp.dot(slopes, tmp[...], preferred_element_type=jnp.float32)
             if side == 0:
                 loss_acc[...] += flag * jnp.sum(jnp.log1p(grown), axis=0, keepdims=True)
 
     def own_item(side):
-        @pl.loop(0, parts)
+        @pl.loop(0, tiles)
         def _(c):
             logits = tile(c, side, own.at[1 - side])
             flag = mask_ref[me, reach].astype(jnp.float32)
             if side == 0:
-                match = pos_col[cut(c), :] == lax.broadcasted_iota(jnp.int32, logits.shape, 1)
+                match = pos_col[band(c), :] == lax.broadcasted_iota(jnp.int32, logits.shape, 1)
             else:
-                match = pos_row[...] == lax.broadcasted_iota(jnp.int32, logits.shape, 0) + c * piece
+                match = pos_row[...] == lax.broadcasted_iota(jnp.int32, logits.shape, 0) + c * tall
             labels = jnp.where(match, 1.0, -1.0)
             grown = jnp.exp(-labels * logits)
             slopes = (-labels * grown / (1.0 + grown) * (scale * flag)).astype(jnp.bfloat16)
-            acc[side, cut(c), :] = jnp.dot(slopes, own[1 - side], preferred_element_type=jnp.float32)
+            acc[side, band(c), :] = jnp.dot(slopes, own[1 - side], preferred_element_type=jnp.float32)
             if side == 0:
                 loss_acc[...] += flag * jnp.sum(jnp.log1p(grown), axis=0, keepdims=True)
+
+    def short_item(which, k):
+        values = got[1, which, band(k), :].astype(jnp.float32)
+        length = jnp.sqrt(jnp.sum(values * values, axis=1, keepdims=True) + epsilon)
+        tmp[0:tall, :] = (values / length).astype(jnp.bfloat16)
+        flag = flag_of(1, which)
+
+        @pl.loop(0, tiles)
+        def _(c):
+            grown = jnp.exp(tile(c, 1, tmp.at[0:tall]))
+            slopes = (grown / (1.0 + grown) * (scale * flag)).astype(jnp.bfloat16)
+            acc[1, band(c), :] += jnp.dot(slopes, tmp[0:tall, :], preferred_element_type=jnp.float32)
+
+    def finish(side, source, result):
+        @pl.loop(0, tiles)
+        def _(c):
+            values = source[band(c), :].astype(jnp.float32)
+            length = jnp.sqrt(jnp.sum(values * values, axis=1, keepdims=True) + epsilon)
+            normed = values / length
+            result[band(c), :] = back_rows(normed, length, acc[side, band(c), :]).astype(result.dtype)
 
     loss_acc[...] = jnp.zeros_like(loss_acc)
     normalise(image_ref, own.at[0])
@@ -266,19 +324,16 @@
         def _():
             forward(OUTER, 1, kind, block(3, 0), c)
 
-        which = first_block(step // 2)
-
-        @pl.when(step % 2 + 0 * role == 0)
-        def _():
-            @pl.when(step < 4 + 2 * role)
-            def _():
-                item(0, which)
-
-        @pl.when(step % 2 == 1)
-        def _():
-            @pl.when(step < 4 + 2 * role)
-            def _():
-                item(1, which)
+        which = first_block(step // 4)
+        wanted = (1 - step % 2) * (role + (1 - role) * (1 - step // 8))
+
+        @pl.when(wanted * (2 - step // 2 % 2) == 2)
+        def _():
+            item(0, which)
+
+        @pl.when(wanted * (1 + step // 2 % 2) == 2)
+        def _():
+            item(1, which)
 
         arrived(kind, block(1 - role, 1), c)
 
@@ -294,35 +349,73 @@
         def _():
             forward(OUTER, 2, kind, block(2, 1), c)
 
-        late = step // 4
-        which = (1 - late) * second_block(step // 2) + late * block(step - 2, 1)
-        busy = 1 - (1 - late) * role * (step // 2)
-
-        @pl.when(busy == 1)
-        def _():
-            @pl.when((1 - late) * (step % 2) == 0)
-            def _():
-                item(0, which)
-
-            @pl.when((1 - late) * (step % 2) == 1)
-            def _():
-                item(1, which)
+        wanted = (1 - (step + 8) // 12) * (1 - role * (step // 2))
+
+        @pl.when(wanted * (2 - step % 2) == 2)
+        def _():
+            item(0, second_block(step // 2))
+
+        @pl.when(wanted * (1 + step % 2) == 2)
+        def _():
+            item(1, second_block(step // 2))
+
+        @pl.when(step == parts)
+        def _():
+            item(0, block(2, 1))
 
         arrived(kind, block(3, 1), c)
 
-    @pl.loop(2, 4)
-    def _(p):
-        item(1, block(p, 1))
-
-    for side, source, result in ((0, image_ref, image_out), (1, text_ref, text_out)):
-        @pl.loop(0, parts)
-        def _(c, side=side, source=source, result=result):
-            values = source[cut(c), :].astype(jnp.float32)
-            length = jnp.sqrt(jnp.sum(values * values, axis=1, keepdims=True) + epsilon)
-            normed = values / length
-            result[cut(c), :] = back_rows(normed, length, acc[side, cut(c), :]).astype(result.dtype)
-
-    loss_out[...] = loss_acc[...]
+        @pl.when(step == parts + 1)
+        def _():
+            item(0, block(3, 1))
+            blk_loss[me] = jnp.full(blk_loss.shape[1:], jnp.sum(loss_acc[...]), jnp.float32)
+
+        @pl.when(step == parts + 2)
+        def _():
+            finish(0, image_ref, image_out)
+
+            @pl.loop(1, count)
+            def _(d):
+                blk_share(d).start()
+
+        @pl.when(step == parts + 3)
+        def _():
+            short_item(block(2, 1), 0)
+            short_item(block(3, 1), 0)
+
+        @pl.when(step == parts + 4)
+        def _():
+            short_item(block(2, 1), 1)
+            short_item(block(3, 1), 1)
+
+    @pl.loop(1, count)
+    def _(d):
+        blk_arrival(d).wait_recv()
+
+    grp_loss[grp] = jnp.sum(blk_loss[...], axis=0)
+    short_item(block(2, 1), 2)
+
+    @pl.loop(1, groups)
+    def _(d):
+        grp_share(d).start()
+
+    short_item(block(3, 1), 2)
+    finish(1, text_ref, text_out)
+
+    @pl.loop(1, groups)
+    def _(d):
+        grp_arrival(d).wait_recv()
+
+    total = jnp.sum(grp_loss[...], axis=0)
+    loss_out[0] = jnp.sum(total[0:1, 0:1]) / (rows * count * groups)
+
+    @pl.loop(1, count)
+    def _(d):
+        blk_share(d).wait_send()
+
+    @pl.loop(1, groups)
+    def _(d):
+        grp_share(d).wait_send()
 
     @pl.loop(0, steps)
     def _(step):
@@ -346,34 +439,41 @@
     row_count, width = image_emb.shape
     if block_count != 2 * (reach + 1) or reach != 3 or row_count % (3 * 128) != 0:
         return plain_body(image_emb, text_emb, positives, pair_mask, log_scale, bias)
-    parts = 3
+    parts, tiles = 6, 3
+    groups = lax.axis_size("grp")
     vmem = pl.BlockSpec(memory_space=pltpu.VMEM)
-    image_grad, text_grad, losses = pl.pallas_call(
-        functools.partial(grid_kernel, reach, parts),
+    smem = pl.BlockSpec(memory_space=pltpu.SMEM)
+    anywhere = pl.BlockSpec(memory_space=pl.ANY)
+    return pl.pallas_call(
+        functools.partial(grid_kernel, reach, parts, tiles),
         out_shape=(
             jax.ShapeDtypeStruct(image_emb.shape, image_emb.dtype),
             jax.ShapeDtypeStruct(text_emb.shape, text_emb.dtype),
-            jax.ShapeDtypeStruct((1, row_count), jnp.float32),
+            jax.ShapeDtypeStruct((1,), jnp.float32),
         ),
-        in_specs=[pl.BlockSpec(memory_space=pltpu.SMEM)] + [vmem] * 6,
-        out_specs=(vmem,) * 3,
+        in_specs=[smem] * 3 + [anywhere] * 2 + [vmem] * 2,
+        out_specs=(vmem, vmem, smem),
         scratch_shapes=[
+            pltpu.VMEM((2, row_count, width), jnp.bfloat16),
             pltpu.VMEM((2, block_count, row_count, width), jnp.bfloat16),
             pltpu.VMEM((2, row_count, width), jnp.bfloat16),
             pltpu.VMEM((row_count, width), jnp.bfloat16),
             pltpu.VMEM((2, row_count, width), jnp.float32),
             pltpu.VMEM((1, row_count), jnp.float32),
+            pltpu.VMEM((block_count, 8, 128), jnp.float32),
+            pltpu.VMEM((groups, 8, 128), jnp.float32),
+            pltpu.SemaphoreType.DMA((2,)),
             pltpu.SemaphoreType.DMA((3, 3, 2, parts)),
             pltpu.SemaphoreType.DMA((2, block_count, parts)),
+            pltpu.SemaphoreType.DMA((block_count,)),
+            pltpu.SemaphoreType.DMA((block_count,)),
+            pltpu.SemaphoreType.DMA((groups,)),
+            pltpu.SemaphoreType.DMA((groups,)),
         ],
         compiler_params=pltpu.CompilerParams(
-            collective_id=0, has_side_effects=True, vmem_limit_bytes=48 * 1024 * 1024
+            collective_id=0, has_side_effects=True, vmem_limit_bytes=56 * 1024 * 1024
         ),
-    )(pair_mask, log_scale.reshape(1, 1), bias.reshape(1, 1), image_emb, text_emb, positives,
-      positives.reshape(row_count, 1))
-    total_loss = lax.psum(jnp.sum(losses), ("blk", "grp"))
-    image_count = row_count * block_count * lax.axis_size("grp")
-    return (image_grad, text_grad, (total_loss / image_count).reshape(1))
+    )(pair_mask, log_scale, bias, image_emb, text_emb, positives, positives.reshape(row_count, 1))
 
 
 def solution(mesh):

time: 188 us -> 146 us (0.78)
  blocking collectives: 38 us -> 0 us
    psum x1 -> x0, blocking collectives: 38 us -> none  [body(): total_loss = lax.psum(jnp.sum(losses), ('blk', 'grp'))]
    unnamed x10 -> x6, local copies, waits for them, and re-layouts: 5.38 us -> 3.16 us
where the time goes in v2:
time: 146 us; the launch traced here: 145 us
  Pallas kernels  138 us (95%)
  local copies, waits for them, and re-layouts  3.98 us (3%)
  between operations  3.66 us (3%)
    pallas_call x1, Pallas kernels, body(): pl.pallas_call(functools.partial(grid_kernel, reach, parts, tiles), out_s...  138 us
    unnamed x6, local copies, waits for them, and re-layouts  3.16 us

profile of v2, /device:TPU:0, one launch (start us, length us, event | category | flops | bytes accessed | tf_op | source)
XLA Modules:
  0.0 145.3 jit_solution(5691046328572760508)
XLA Ops:
  1.3 0.0 copy-start.1
  1.9 0.0 copy-done.1
  2.0 0.8 copy.9.pos_col
  2.8 137.7 %shard_map.85 = (bf16[384,1152]{1,0:T(8,128)(2,1)}, bf16[384,1152]{1,0:T(8,128)(2,1)}, f32[1]{0:T(128)}) custom-call(s32[8,7]{1,0:T(8,128)} %mask_ref.1, f32[1]{0:T(128)S(6)} %copy.13.scale_ref, f32[1]{0:T(128)S(6)} %copy.14.offset_ref, bf16[384,1152]{1,0:T(8,128)(2,1)} %image_hbm.1, bf16[384,1152]{1,0:T(8,128)(2,1)} %text_hbm.1, s32[1,384]{1,0:T(1,128)} %pos_row.1, ...), custom_call_target="tpu_custom_call" | custom-call | tf_op jit(solution)/shard_map/pallas_call | solution.py:447
  140.5 0.0 copy-start
  140.5 2.2 %copy.15 = bf16[384,1152]{1,0:T(8,128)(2,1)} copy(bf16[384,1152]{1,0:T(8,128)(2,1)} %get-tuple-element.6) | data formatting | bytes 1769472
  142.7 0.0 copy-done
  142.7 0.9 copy.16
Async XLA Ops:
  1.3 0.7 copy-start.1
  140.5 2.2 %copy-start = (bf16[384,1152]{1,0:T(8,128)(2,1)S(1)}, bf16[384,1152]{1,0:T(8,128)(2,1)}, u32[]{:S(2)}) copy-start(bf16[384,1152]{1,0:T(8,128)(2,1)} %get-tuple-element.7) | copy-start | bytes 2654212

commit v3 on v2

--- a/solution.py
+++ b/solution.py
@@ -102,10 +102,10 @@
 Y, INNER, OUTER = 0, 1, 2
 
 
-def grid_kernel(reach, parts, tiles, mask_ref, scale_ref, offset_ref, image_hbm, text_hbm, pos_row, pos_col,
+def grid_kernel(reach, parts, tiles, mask_ref, scale_ref, offset_ref, image_hbm, text_hbm, pos_hbm,
                 image_out, text_out, loss_out,
-                held, got, own, tmp, acc, loss_acc, blk_loss, grp_loss,
-                load_sem, send_sem, recv_sem, blk_send, blk_recv, grp_send, grp_recv):
+                held, pos_row, ready, got, own, tmp, acc, loss_acc, blk_loss, grp_loss,
+                load_sem, out_sem, send_sem, recv_sem, blk_send, blk_recv, grp_send, grp_recv):
     me = lax.axis_index("blk")
     grp = lax.axis_index("grp")
     count = lax.axis_size("blk")
@@ -151,6 +151,7 @@
         pltpu.make_async_copy(source, held.at[kind], load_sem.at[kind])
         for kind, source in ((0, text_hbm), (1, image_hbm))
     ]
+    loads.append(pltpu.make_async_copy(pos_hbm, pos_row, load_sem.at[2]))
     for load in loads:
         load.start()
     barrier = pltpu.get_barrier_semaphore()
@@ -241,10 +242,11 @@
             logits = tile(c, side, own.at[1 - side])
             flag = mask_ref[me, reach].astype(jnp.float32)
             if side == 0:
-                match = pos_col[band(c), :] == lax.broadcasted_iota(jnp.int32, logits.shape, 1)
+                hit = pos_row[:, band(c)] == lax.broadcasted_iota(jnp.int32, (rows, tall), 0)
+                labels = jnp.transpose(jnp.where(hit, 1.0, -1.0))
             else:
-                match = pos_row[...] == lax.broadcasted_iota(jnp.int32, logits.shape, 0) + c * tall
-            labels = jnp.where(match, 1.0, -1.0)
+                hit = pos_row[...] == lax.broadcasted_iota(jnp.int32, logits.shape, 0) + c * tall
+                labels = jnp.where(hit, 1.0, -1.0)
             grown = jnp.exp(-labels * logits)
             slopes = (-labels * grown / (1.0 + grown) * (scale * flag)).astype(jnp.bfloat16)
             acc[side, band(c), :] = jnp.dot(slopes, own[1 - side], preferred_element_type=jnp.float32)
@@ -262,6 +264,9 @@
             grown = jnp.exp(tile(c, 1, tmp.at[0:tall]))
             slopes = (grown / (1.0 + grown) * (scale * flag)).astype(jnp.bfloat16)
             acc[1, band(c), :] += jnp.dot(slopes, tmp[0:tall, :], preferred_element_type=jnp.float32)
+
+    def put_out(side, result, c):
+        return pltpu.make_async_copy(ready.at[side, band(c)], result.at[band(c)], out_sem.at[side, c])
 
     def finish(side, source, result):
         @pl.loop(0, tiles)
@@ -269,8 +274,10 @@
             values = source[band(c), :].astype(jnp.float32)
             length = jnp.sqrt(jnp.sum(values * values, axis=1, keepdims=True) + epsilon)
             normed = values / length
-            result[band(c), :] = back_rows(normed, length, acc[side, band(c), :]).astype(result.dtype)
-
+            ready[side, band(c), :] = back_rows(normed, length, acc[side, band(c), :]).astype(ready.dtype)
+            put_out(side, result, c).start()
+
+    loads[2].wait()
     loss_acc[...] = jnp.zeros_like(loss_acc)
     normalise(image_ref, own.at[0])
     normalise(text_ref, own.at[1])
@@ -340,7 +347,7 @@
     def second_block(i):
         return block((1 - role) * (3 - 2 * i), (1 - role) * i + role)
 
-    @pl.loop(0, steps)
+    @pl.loop(0, steps - 1)
     def _(step):
         kind, c = step // parts, step % parts
         arrived(kind, block(2, 1), c)
@@ -388,25 +395,43 @@
             short_item(block(2, 1), 1)
             short_item(block(3, 1), 1)
 
+    final = role * 0 + parts - 1
+
+    @pl.when(is_mid)
+    def _():
+        arrived(1, block(2, 1), final)
+        forward(OUTER, 2, 1, block(2, 1), final)
+
+    arrived(1, block(3, 1), final)
+
     @pl.loop(1, count)
     def _(d):
         blk_arrival(d).wait_recv()
 
     grp_loss[grp] = jnp.sum(blk_loss[...], axis=0)
+    short_item(block(3, 1), 2)
+
+    @pl.loop(1, groups)
+    def _(d):
+        grp_share(d).start()
+
+    @pl.when(is_end)
+    def _():
+        arrived(1, block(2, 1), final)
+
     short_item(block(2, 1), 2)
+    finish(1, text_ref, text_out)
 
     @pl.loop(1, groups)
     def _(d):
-        grp_share(d).start()
-
-    short_item(block(3, 1), 2)
-    finish(1, text_ref, text_out)
-
-    @pl.loop(1, groups)
-    def _(d):
         grp_arrival(d).wait_recv()
 
     total = jnp.sum(grp_loss[...], axis=0)
+    @pl.loop(0, tiles)
+    def _(c):
+        put_out(0, image_out, c).wait()
+        put_out(1, text_out, c).wait()
+
     loss_out[0] = jnp.sum(total[0:1, 0:1]) / (rows * count * groups)
 
     @pl.loop(1, count)
@@ -441,7 +466,6 @@
         return plain_body(image_emb, text_emb, positives, pair_mask, log_scale, bias)
     parts, tiles = 6, 3
     groups = lax.axis_size("grp")
-    vmem = pl.BlockSpec(memory_space=pltpu.VMEM)
     smem = pl.BlockSpec(memory_space=pltpu.SMEM)
     anywhere = pl.BlockSpec(memory_space=pl.ANY)
     return pl.pallas_call(
@@ -451,9 +475,11 @@
             jax.ShapeDtypeStruct(text_emb.shape, text_emb.dtype),
             jax.ShapeDtypeStruct((1,), jnp.float32),
         ),
-        in_specs=[smem] * 3 + [anywhere] * 2 + [vmem] * 2,
-        out_specs=(vmem, vmem, smem),
+        in_specs=[smem] * 3 + [anywhere] * 3,
+        out_specs=(anywhere, anywhere, smem),
         scratch_shapes=[
+            pltpu.VMEM((2, row_count, width), jnp.bfloat16),
+            pltpu.VMEM((1, row_count), jnp.int32),
             pltpu.VMEM((2, row_count, width), jnp.bfloat16),
             pltpu.VMEM((2, block_count, row_count, width), jnp.bfloat16),
             pltpu.VMEM((2, row_count, width), jnp.bfloat16),
@@ -462,7 +488,8 @@
             pltpu.VMEM((1, row_count), jnp.float32),
             pltpu.VMEM((block_count, 8, 128), jnp.float32),
             pltpu.VMEM((groups, 8, 128), jnp.float32),
-            pltpu.SemaphoreType.DMA((2,)),
+            pltpu.SemaphoreType.DMA((3,)),
+            pltpu.SemaphoreType.DMA((2, tiles)),
             pltpu.SemaphoreType.DMA((3, 3, 2, parts)),
             pltpu.SemaphoreType.DMA((2, block_count, parts)),
             pltpu.SemaphoreType.DMA((block_count,)),
@@ -471,9 +498,9 @@
             pltpu.SemaphoreType.DMA((groups,)),
         ],
         compiler_params=pltpu.CompilerParams(
-            collective_id=0, has_side_effects=True, vmem_limit_bytes=56 * 1024 * 1024
+            collective_id=0, has_side_effects=True, vmem_limit_bytes=67043328
         ),
-    )(pair_mask, log_scale, bias, image_emb, text_emb, positives, positives.reshape(row_count, 1))
+    )(pair_mask, log_scale, bias, image_emb, text_emb, positives)
 
 
 def solution(mesh):

time: 146 us -> 144 us (0.986)
    unnamed x6 -> x4, local copies, waits for them, and re-layouts: 3.16 us -> 3.14 us
where the time goes in v3:
time: 144 us
  Pallas kernels  137 us (95%)
  between operations  3.76 us (3%)
  local copies, waits for them, and re-layouts  3.14 us (2%)
    pallas_call x1, Pallas kernels, body(): pl.pallas_call(functools.partial(grid_kernel, reach, parts, tiles), out_s...  137 us
    unnamed x4, local copies, waits for them, and re-layouts  3.14 us

profile of v3, /device:TPU:0, one launch (start us, length us, event | category | flops | bytes accessed | tf_op | source)
XLA Modules:
  0.0 143.8 jit_solution(15389756159213953539)
XLA Ops:
  1.9 136.9 %shard_map.85 = (bf16[384,1152]{1,0:T(8,128)(2,1)}, bf16[384,1152]{1,0:T(8,128)(2,1)}, f32[1]{0:T(128)}) custom-call(s32[8,7]{1,0:T(8,128)} %mask_ref.1, f32[1]{0:T(128)S(6)} %copy.12.scale_ref, f32[1]{0:T(128)S(6)} %copy.13.offset_ref, bf16[384,1152]{1,0:T(8,128)(2,1)} %image_hbm.1, bf16[384,1152]{1,0:T(8,128)(2,1)} %text_hbm.1, s32[1,384]{1,0:T(1,128)} %pos_hbm.1), custom_call_target="tpu_custom_call" | custom-call | tf_op jit(solution)/shard_map/pallas_call | solution.py:471
  138.9 0.0 copy-start
  138.9 2.2 %copy.14 = bf16[384,1152]{1,0:T(8,128)(2,1)} copy(bf16[384,1152]{1,0:T(8,128)(2,1)} %get-tuple-element.6) | data formatting | bytes 1769472
  141.1 0.0 copy-done
  141.1 0.9 copy.15
Async XLA Ops:
  138.9 2.2 %copy-start = (bf16[384,1152]{1,0:T(8,128)(2,1)S(1)}, bf16[384,1152]{1,0:T(8,128)(2,1)}, u32[]{:S(2)}) copy-start(bf16[384,1152]{1,0:T(8,128)(2,1)} %get-tuple-element.7) | copy-start | bytes 2654212
